TPU v7x, 32 devices: a whole 2x2x4 slice. The times are simulated.
32 devices in a mesh: head: 2 (over y), seq: 16 (over z, x, core).
Axes of the slice: x: 2, y: 2, z: 4, core: 2. Of those that a mesh axis runs over, the one named last changes fastest.
Arguments:
- queries: bfloat16 [2048, 4096], P(('seq', 'head')), may hold values from -20 to 20
- keys: bfloat16 [2048, 1024], P(('seq', 'head')), may hold values from -5 to 5
- values: bfloat16 [2048, 1024], P(('seq', 'head')), may hold values from -6 to 6
Outputs:
- attended: bfloat16 [2048, 4096], P(('seq', 'head'))
All inputs are finite; a program needn't handle non-finite values.
Results may differ from a plain program's by a relative error of at most 0.0041.
Values may be sent and summed in bfloat16 or wider, within the bound.
No kernel may reach another device: no remote copies, remote signals or barrier semaphores. Data moves between devices by JAX's collectives and lax.ppermute only.
A program may use at most 64 MiB of HBM per device.

v0:
```python
import math
import jax
import jax.numpy as jnp
from jax import lax
from jax.sharding import PartitionSpec as P

HEAD_DIM = 128


def update_state(state, query_half, query_pos, key_piece, value_piece, key_pos):
    largest, total, summed = state
    score = jnp.einsum("tkgd,pkd->tkgp", query_half, key_piece, preferred_element_type=jnp.float32)
    score = score / math.sqrt(query_half.shape[-1])
    allowed = (key_pos[None, :] <= query_pos[:, None])[:, None, None, :]
    score = jnp.where(allowed, score, jnp.float32(-1e30))
    new_largest = jnp.maximum(largest, jnp.max(score, axis=-1))
    weight = jnp.where(allowed, jnp.exp(score - new_largest[..., None]), jnp.float32(0.0))
    total = jnp.sum(weight, axis=-1)
    product = jnp.einsum(
        "tkgp,pkd->tkgd",
        weight.astype(jnp.bfloat16),
        value_piece,
        preferred_element_type=jnp.float32,
    )
    summed = product
    return (new_largest, total, summed)


def on_device(queries, keys, values):
    q_local, k_local, v_local = (
        lax.all_to_all(queries, "head", split_axis=1, concat_axis=0, tiled=True),
        lax.all_to_all(keys, "head", split_axis=1, concat_axis=0, tiled=True),
        lax.all_to_all(values, "head", split_axis=1, concat_axis=0, tiled=True),
    )
    tokens = q_local.shape[0]
    half = tokens // 2
    kv_local = k_local.shape[1] // HEAD_DIM
    group = q_local.shape[1] // k_local.shape[1]
    index = lax.axis_index("seq")
    offsets = jnp.arange(half, dtype=jnp.int32)
    later = q_local[half:]
    early_pos = index * tokens + offsets
    later_pos = index * tokens + half + offsets
    query_pos = jnp.stack([early_pos, later_pos])
    halves = jnp.stack([q_local[:half], later]).reshape(2, half, kv_local, group, HEAD_DIM)
    start_state = (
        jnp.full((2, half, kv_local, group), -1e30, jnp.float32),
        jnp.zeros((2, half, kv_local, group), jnp.float32),
        jnp.zeros((2, half, kv_local, group, HEAD_DIM), jnp.float32),
    )
    start = jnp.int32(0)
    key_piece = lax.all_gather(k_local, "seq", axis=0, tiled=True)
    value_piece = lax.all_gather(v_local, "seq", axis=0, tiled=True)
    rows = key_piece.shape[0]
    key_piece = key_piece.reshape(rows, kv_local, HEAD_DIM)
    value_piece = value_piece.reshape(rows, kv_local, HEAD_DIM)
    key_pos = jnp.arange(rows, dtype=jnp.int32)
    results = []
    for which in range(2):
        state = (start_state[0][which], start_state[1][which], start_state[2][which])
        needed = start <= query_pos[which, half - 1]

        def run(current, which=which):
            return update_state(
                current, halves[which], query_pos[which], key_piece, value_piece, key_pos
            )

        def keep(current):
            return current

        results.append(lax.cond(needed, run, keep, state))
    total = jnp.stack([results[0][1], results[1][1]])
    summed = jnp.stack([results[0][2], results[1][2]])
    result = (summed / total[..., None]).reshape(2, half, q_local.shape[1]).astype(jnp.bfloat16)
    later_out = result[1]
    combined = jnp.concatenate([result[0], later_out], axis=0)
    return lax.all_to_all(combined, "head", split_axis=0, concat_axis=1, tiled=True)


def solution(mesh):
    return jax.shard_map(
        on_device,
        mesh=mesh,
        in_specs=(P(("seq", "head"), None), P(("seq", "head"), None), P(("seq", "head"), None)),
        out_specs=P(("seq", "head"), None),
        check_vma=False,
    )
```

profile of v0, /device:TPU:0, one launch (start us, length us, event | category | flops | bytes accessed | tf_op | source)
XLA Modules:
  0.0 142.9 jit_solution(106555980706747682)
XLA Ops:
  6.5 0.0 all-gather.3.cloned.1.call-start
  6.5 0.9 copy.81
  7.5 8.6 %all_to_all.73 = bf16[64,2,512]{2,0,1:T(8,128)(2,1)} all-to-all(bf16[64,2,512]{2,0,1:T(8,128)(2,1)S(1)} %bitcast.111), channel_id=1, replica_groups=mesh['head'=2,'seq'=16] {'head'}, dimensions={1} | all-to-all | bytes 262144 | tf_op jit(solution)/shard_map/all_to_all | solution.py:32
  16.1 0.0 all-gather.3.cloned.1.call-update
  16.1 0.0 all-gather.5.cloned.1.call-start
  16.2 0.9 copy.80
  17.1 7.5 %all_to_all.74 = bf16[64,2,512]{2,0,1:T(8,128)(2,1)} all-to-all(bf16[64,2,512]{2,0,1:T(8,128)(2,1)S(1)} %bitcast.112), channel_id=1, replica_groups=mesh['head'=2,'seq'=16] {'head'}, dimensions={1} | all-to-all | bytes 262144 | tf_op jit(solution)/shard_map/all_to_all | solution.py:33
  24.6 0.0 all-gather.5.cloned.1.call-update
  24.6 1.9 %copy.79 = bf16[8,2,8,2048]{3,2,0,1:T(8,128)(2,1)} copy(bf16[8,2,8,2048]{3,2,1,0:T(8,128)(2,1)} %bitcast.108) | data formatting | bytes 1048576 | tf_op jit(solution)/shard_map/all_to_all | solution.py:31
  26.5 3.5 %all-to-all-start = ((bf16[64,2,2048]{2,0,1:T(8,128)(2,1)}), bf16[64,2,2048]{2,0,1:T(8,128)(2,1)S(1)}, u32[]{:S(2)}, u32[]{:S(2)}) async-start(bf16[64,2,2048]{2,0,1:T(8,128)(2,1)} %bitcast.98), calls=%async_computation | async-start | bytes 1048576 | tf_op jit(solution)/shard_map/all_to_all | solution.py:31
  30.0 0.6 slice.29
  31.4 0.6 slice.26
  32.6 4.0 %all-to-all-done = bf16[64,2,2048]{2,0,1:T(8,128)(2,1)S(1)} async-done(((bf16[64,2,2048]{2,0,1:T(8,128)(2,1)}), bf16[64,2,2048]{2,0,1:T(8,128)(2,1)S(1)}, u32[]{:S(2)}, u32[]{:S(2)}) %all-to-all-start) | async-done | bytes 524320 | tf_op jit(solution)/shard_map/all_to_all | solution.py:31
  36.6 0.2 stack.42
  36.8 0.2 stack.41
  37.0 0.1 constant_dynamic-update-slice_fusion.1
  37.1 0.1 constant_dynamic-update-slice_fusion
  37.2 21.2 %all-gather.3.cloned.1.call-done = bf16[2048,512]{1,0:T(8,128)(2,1)} async-done(((bf16[128,512]{1,0:T(8,128)(2,1)}), bf16[2048,512]{1,0:T(8,128)(2,1)}) %all-gather.3.cloned.1.call-update) | async-done | bytes 2097168 | tf_op jit(solution)/shard_map/all_gather | solution.py:52
  58.4 2.9 %copy.49 = bf16[2048,512]{0,1:T(8,128)(2,1)S(1)} copy(bf16[2048,512]{1,0:T(8,128)(2,1)} %all-gather.3.cloned.1.call-done) | data formatting | bytes 4194304 | tf_op jit(solution)/shard_map/all_gather | solution.py:52
  61.3 39.4 %all-gather.5.cloned.1.call-done = bf16[2048,512]{1,0:T(8,128)(2,1)} async-done(((bf16[128,512]{1,0:T(8,128)(2,1)}), bf16[2048,512]{1,0:T(8,128)(2,1)}) %all-gather.5.cloned.1.call-update) | async-done | bytes 2097168 | tf_op jit(solution)/shard_map/all_gather | solution.py:53
  100.7 4.0 %copy.51 = bf16[2048,512]{0,1:T(8,128)(2,1)} copy(bf16[2048,512]{1,0:T(8,128)(2,1)} %all-gather.5.cloned.1.call-done) | data formatting | bytes 4194304 | tf_op jit(solution)/shard_map/all_gather | solution.py:53
  104.7 8.9 %conditional.2 = (f32[1,64,4,4]{1,3,2,0:T(4,128)S(1)}, f32[1,64,2048]{2,1,0:T(8,128)S(1)}) conditional(s32[]{:T(128)} %bitcast.12, () %tuple.29, (s32[2048]{0:T(1024)S(1)}, s32[]{:T(128)}, s32[64]{0:T(128)S(1)}, bf16[2,64,4,4,128]{4,3,2,1,0:T(4,128)(2,1)S(1)}, bf16[2048,4,128]{0,2,1:T(8,128)(2,1)S(1)}, ...), branch_computations={%region_0.0_spmd, %region_1.4_spmd} | conditional | flops 1101134848 | bytes 42238768 | solution.py:71
  104.8 0.1 broadcast_compare_fusion
  104.9 0.1 copy.52
  105.0 0.0 copy-start
  105.1 1.7 %fusion = (f32[64,4,4]{0,2,1:T(4,128)S(1)}, f32[4,2048,64,4]{1,2,3,0:T(8,128)S(1)}) fusion(pred[64,2048]{1,0:T(8,128)(4,1)S(1)} %broadcast_compare_fusion, bf16[2,64,4,4,128]{4,1,3,2,0:T(8,128)(2,1)S(1)} %copy.52, bf16[2048,4,128]{0,2,1:T(8,128)(2,1)S(1)} %get-tuple-element.97), kind=kOutput, calls=%fused_computation.2 | convolution fusion | flops 543161344 | bytes 10883072 | tf_op jit(solution)/shard_map/cond/branch_1_fun/tkgd,pkd->tkgp/dot_general | solution.py:12
  106.7 0.0 copy-done
  106.8 1.9 %fusion.9 = f32[64,4,4,128]{3,0,2,1:T(8,128)S(1)} fusion(bf16[2048,4,128]{0,2,1:T(8,128)(2,1)S(1)} %copy-done, f32[4,2048,64,4]{1,2,3,0:T(8,128)S(1)} %get-tuple-element.106, f32[64,4,4]{0,2,1:T(4,128)S(1)} %broadcast_maximum_fusion, pred[64,2048]{1,0:T(8,128)(4,1)S(1)} %broadcast_compare_fusion), kind=kOutput, calls=%fused_computation.10 | convolution fusion | flops 547356672 | bytes 11145216 | tf_op jit(solution)/shard_map/cond/branch_1_fun/tkgp,pkd->tkgd/dot_general | solution.py:19
  108.7 2.5 %fusion.2 = f32[64,4,4]{0,2,1:T(4,128)S(1)} fusion(f32[4,2048,64,4]{1,2,3,0:T(8,128)S(1)} %get-tuple-element.106, f32[64,4,4]{0,2,1:T(4,128)S(1)} %broadcast_maximum_fusion, pred[64,2048]{1,0:T(8,128)(4,1)S(1)} %broadcast_compare_fusion), kind=kLoop, calls=%fused_computation.4 | loop fusion | flops 10484736 | bytes 8527872 | tf_op jit(solution)/shard_map/cond/branch_1_fun/reduce_sum | solution.py:18
  111.2 1.1 copy.45
  112.4 1.3 stack.31
  113.6 8.0 %conditional.3 = (f32[1,64,4,4]{1,3,2,0:T(4,128)S(1)}, f32[1,64,2048]{2,1,0:T(8,128)}) conditional(s32[]{:T(128)} %bitcast.20, () %tuple.31, (s32[2048]{0:T(1024)S(1)}, s32[]{:T(128)}, s32[64]{0:T(128)S(1)}, bf16[2,64,4,4,128]{4,3,2,1,0:T(4,128)(2,1)S(1)}, bf16[2048,4,128]{0,2,1:T(8,128)(2,1)S(1)}, /*index=5*/bf16[2048,4,128]{0,2,1:T(8,128)(2,1)}) %tuple.56), branch_computations={%region_4.5_spmd, %region_5.8_spmd} | conditional | flops 1101134848 | bytes 42238768 | solution.py:71
  113.8 0.1 broadcast_compare_fusion.1
  114.0 0.1 copy.55
  114.1 0.0 copy-start.1
  114.1 1.7 %fusion.17 = (f32[64,4,4]{0,2,1:T(4,128)S(1)}, f32[4,2048,64,4]{1,2,3,0:T(8,128)S(1)}) fusion(pred[64,2048]{1,0:T(8,128)(4,1)S(1)} %broadcast_compare_fusion.1, bf16[2,64,4,4,128]{4,1,3,2,0:T(8,128)(2,1)S(1)} %copy.55, bf16[2048,4,128]{0,2,1:T(8,128)(2,1)S(1)} %get-tuple-element.103), kind=kOutput, calls=%fused_computation.20 | convolution fusion | flops 543161344 | bytes 10883072 | tf_op jit(solution)/shard_map/cond/branch_1_fun/tkgd,pkd->tkgp/dot_general | solution.py:12
  115.8 0.0 copy-done.1
  115.8 1.9 %fusion.26 = f32[64,4,4,128]{3,0,2,1:T(8,128)S(1)} fusion(bf16[2048,4,128]{0,2,1:T(8,128)(2,1)S(1)} %copy-done.1, f32[4,2048,64,4]{1,2,3,0:T(8,128)S(1)} %get-tuple-element.108, f32[64,4,4]{0,2,1:T(4,128)S(1)} %broadcast_maximum_fusion.1, pred[64,2048]{1,0:T(8,128)(4,1)S(1)} %broadcast_compare_fusion.1), kind=kOutput, calls=%fused_computation.28 | convolution fusion | flops 547356672 | bytes 11145216 | tf_op jit(solution)/shard_map/cond/branch_1_fun/tkgp,pkd->tkgd/dot_general | solution.py:19
  117.8 2.5 %fusion.19 = f32[64,4,4]{0,2,1:T(4,128)S(1)} fusion(f32[4,2048,64,4]{1,2,3,0:T(8,128)S(1)} %get-tuple-element.108, f32[64,4,4]{0,2,1:T(4,128)S(1)} %broadcast_maximum_fusion.1, pred[64,2048]{1,0:T(8,128)(4,1)S(1)} %broadcast_compare_fusion.1), kind=kLoop, calls=%fused_computation.22 | loop fusion | flops 10484736 | bytes 8527872 | tf_op jit(solution)/shard_map/cond/branch_1_fun/reduce_sum | solution.py:18
  120.3 0.3 copy.46
  120.7 1.0 stack.35
  121.7 0.2 copy.58
  121.9 0.6 div.21
  122.5 0.4 div.22
  122.9 1.2 fusion.34
  124.2 11.1 %all_to_all.75 = bf16[2,64,2048]{2,1,0:T(8,128)(2,1)S(1)} all-to-all(bf16[2,64,2048]{2,1,0:T(8,128)(2,1)S(1)} %bitcast.106), channel_id=1, replica_groups=mesh['head'=2,'seq'=16] {'head'}, dimensions={0} | all-to-all | bytes 1048576 | tf_op jit(solution)/shard_map/all_to_all | solution.py:77
  135.2 0.8 copy.75
  (14 shorter events, 0.2 us)
Async XLA Ops:
  6.5 51.8 %all-gather.3.cloned.1.call-start = ((), (), s32[]{:S(2)}) async-start(), calls=%async_computation.4 | async-start | bytes 2228224 | tf_op jit(solution)/shard_map/all_gather | solution.py:52
  16.1 84.6 %all-gather.5.cloned.1.call-start = ((), (), s32[]{:S(2)}) async-start(), calls=%async_computation.5 | async-start | bytes 2228224 | tf_op jit(solution)/shard_map/all_gather | solution.py:53
  26.5 10.1 %all-to-all-start = ((bf16[64,2,2048]{2,0,1:T(8,128)(2,1)}), bf16[64,2,2048]{2,0,1:T(8,128)(2,1)S(1)}, u32[]{:S(2)}, u32[]{:S(2)}) async-start(bf16[64,2,2048]{2,0,1:T(8,128)(2,1)} %bitcast.98), calls=%async_computation | async-start | bytes 1048576 | tf_op jit(solution)/shard_map/all_to_all | solution.py:31
  105.0 1.7 %copy-start = (bf16[2048,4,128]{0,2,1:T(8,128)(2,1)S(1)}, bf16[2048,4,128]{0,2,1:T(8,128)(2,1)}, u32[]{:S(2)}) copy-start(bf16[2048,4,128]{0,2,1:T(8,128)(2,1)} %get-tuple-element.98) | copy-start | bytes 6291460 | tf_op jit(solution)/shard_map/cond
  114.1 1.7 %copy-start.1 = (bf16[2048,4,128]{0,2,1:T(8,128)(2,1)S(1)}, bf16[2048,4,128]{0,2,1:T(8,128)(2,1)}, u32[]{:S(2)}) copy-start(bf16[2048,4,128]{0,2,1:T(8,128)(2,1)} %get-tuple-element.104) | copy-start | bytes 6291460 | tf_op jit(solution)/shard_map/cond
Sparse Core Ops, SparseCore 0:
  16.2 42.0 all-gather.2
  60.5 40.1 all-gather.4
where the time goes:
time: 144 us; the launch traced here: 143 us
  waiting for transfers between devices  64.6 us (45%)
  blocking collectives  27.2 us (19%)
  local copies, waits for them, and re-layouts  18.5 us (13%)
  between operations  14.8 us (10%)
  matrix products  7.21 us (5%)
  other arithmetic  6.63 us (5%)
  starting transfers between devices  3.53 us (2%)
    all_gather x1, waiting for transfers between devices, on_device(): value_piece = lax.all_gather(v_local, 'seq', axis=0, tiled=True)  39.4 us
    all_gather x1, waiting for transfers between devices, on_device(): key_piece = lax.all_gather(k_local, 'seq', axis=0, tiled=True)  21.2 us
    all_to_all x1, blocking collectives, on_device(): lax.all_to_all(combined, 'head', split_axis=0, concat_axis=1, tiled=True)  11.1 us
    all_to_all x1, blocking collectives, on_device(): lax.all_to_all(keys, 'head', split_axis=1, concat_axis=0, tiled=True)  8.64 us
    all_to_all x1, blocking collectives, on_device(): lax.all_to_all(values, 'head', split_axis=1, concat_axis=0, tiled=True)  7.52 us
    reduce_sum x2, other arithmetic, update_state(): total = jnp.sum(weight, axis=-1)  5.08 us
    all_to_all x1, waiting for transfers between devices, on_device(): lax.all_to_all(queries, 'head', split_axis=1, concat_axis=0, tiled=True)  3.99 us
    all_gather x1, local copies, waits for them, and re-layouts, on_device(): value_piece = lax.all_gather(v_local, 'seq', axis=0, tiled=True)  3.95 us
  transfers between devices with their start and end apart: 3, of which 3 were waited for; matrix products, arithmetic and copies ran while one was open for 5% of the time, Pallas kernels for 0%

commit v1 on v0

--- a/solution.py
+++ b/solution.py
@@ -5,6 +5,16 @@
 from jax.sharding import PartitionSpec as P
 
 HEAD_DIM = 128
+
+
+def pass_along(block, name, dim):
+    size = lax.axis_size(name)
+    current, shards = (block, [block])
+    for _ in range(size - 1):
+        current = lax.ppermute(current, name, [(i, (i + 1) % size) for i in range(size)])
+        shards.insert(0, current)
+    merged = jnp.concatenate(shards, axis=dim)
+    return jnp.roll(merged, (lax.axis_index(name) + 1) * block.shape[dim], axis=dim)
 
 
 def update_state(state, query_half, query_pos, key_piece, value_piece, key_pos):
@@ -49,7 +59,7 @@
         jnp.zeros((2, half, kv_local, group, HEAD_DIM), jnp.float32),
     )
     start = jnp.int32(0)
-    key_piece = lax.all_gather(k_local, "seq", axis=0, tiled=True)
+    key_piece = pass_along(k_local, "seq", 0)
     value_piece = lax.all_gather(v_local, "seq", axis=0, tiled=True)
     rows = key_piece.shape[0]
     key_piece = key_piece.reshape(rows, kv_local, HEAD_DIM)

time: 144 us -> 198 us (1.38)
  waiting for transfers between devices: 64.6 us -> 120 us
  blocking collectives: 27.2 us -> 19.6 us
  starting transfers between devices: 3.53 us -> 7 us
  local copies, waits for them, and re-layouts: 18.5 us -> 20.9 us
    ppermute x0 -> x15, waiting for transfers between devices: none -> 97.3 us  [pass_along(): lax.ppermute(current, name, [(i, (i + 1) % size) for i in range(size)])]
    all_gather x1 -> x0, waiting for transfers between devices: 21.2 us -> none  [on_device(): key_piece = lax.all_gather(k_local, 'seq', axis=0, tiled=True)]
    all_gather x1, waiting for transfers between devices: 39.4 us -> 19.6 us  [on_device(): value_piece = lax.all_gather(v_local, 'seq', axis=0, tiled=True)]
    all_to_all x1 -> x0, blocking collectives: 7.52 us -> none  [on_device(): lax.all_to_all(values, 'head', split_axis=1, concat_axis=0, tiled=True)]
    dynamic_slice x0 -> x2, local copies, waits for them, and re-layouts: none -> 4.4 us  [pass_along(): jnp.roll(merged, (lax.axis_index(name) + 1) * block.shape[dim], axis=dim)]
    all_to_all x1, waiting for transfers between devices: 3.99 us -> 0.01 us  [on_device(): lax.all_to_all(queries, 'head', split_axis=1, concat_axis=0, tiled=True)]
    all_to_all x0 -> x1, starting transfers between devices: none -> 3.38 us  [on_device(): lax.all_to_all(values, 'head', split_axis=1, concat_axis=0, tiled=True)]
    all_to_all x0 -> x1, waiting for transfers between devices: none -> 3.17 us  [on_device(): lax.all_to_all(values, 'head', split_axis=1, concat_axis=0, tiled=True)]
  transfers between devices with their start and end apart: 3 -> 18, of which waited for: 3 -> 16; matrix products, arithmetic and copies ran while one was open for 5% -> 5% of each run, Pallas kernels for 0% -> 0%
where the time goes in v1:
time: 198 us; the launch traced here: 197 us
  waiting for transfers between devices  120 us (61%)
  local copies, waits for them, and re-layouts  20.9 us (11%)
  blocking collectives  19.6 us (10%)
  between operations  15.1 us (8%)
  matrix products  7.21 us (4%)
  starting transfers between devices  7 us (4%)
  other arithmetic  6.63 us (3%)
    ppermute x15, waiting for transfers between devices, pass_along(): lax.ppermute(current, name, [(i, (i + 1) % size) for i in range(size)])  97.3 us
    all_gather x1, waiting for transfers between devices, on_device(): value_piece = lax.all_gather(v_local, 'seq', axis=0, tiled=True)  19.6 us
    all_to_all x1, blocking collectives, on_device(): lax.all_to_all(combined, 'head', split_axis=0, concat_axis=1, tiled=True)  11.1 us
    all_to_all x1, blocking collectives, on_device(): lax.all_to_all(keys, 'head', split_axis=1, concat_axis=0, tiled=True)  8.54 us
    reduce_sum x2, other arithmetic, update_state(): total = jnp.sum(weight, axis=-1)  5.08 us
    dynamic_slice x2, local copies, waits for them, and re-layouts, pass_along(): jnp.roll(merged, (lax.axis_index(name) + 1) * block.shape[dim], axis=dim)  4.4 us
    all_gather x1, local copies, waits for them, and re-layouts, on_device(): value_piece = lax.all_gather(v_local, 'seq', axis=0, tiled=True)  3.97 us
  transfers between devices with their start and end apart: 18, of which 16 were waited for; matrix products, arithmetic and copies ran while one was open for 5% of the time, Pallas kernels for 0%

profile of v1, /device:TPU:0, one launch (start us, length us, event | category | flops | bytes accessed | tf_op | source)
XLA Modules:
  0.0 196.9 jit_solution(14367997923555917838)
XLA Ops:
  6.5 0.9 copy.81
  7.5 8.5 %all_to_all.73 = bf16[64,2,512]{2,0,1:T(8,128)(2,1)S(1)} all-to-all(bf16[64,2,512]{2,0,1:T(8,128)(2,1)S(1)} %bitcast.113), channel_id=1, replica_groups=mesh['head'=2,'seq'=16] {'head'}, dimensions={1} | all-to-all | bytes 262144 | tf_op jit(solution)/shard_map/all_to_all | solution.py:42
  16.0 7.1 %collective-permute-done = bf16[128,512]{1,0:T(8,128)(2,1)S(1)} collective-permute-done((bf16[128,512]{1,0:T(8,128)(2,1)S(1)}, bf16[128,512]{1,0:T(8,128)(2,1)S(1)}, u32[]{:S(2)}, u32[]{:S(2)}) %collective-permute-start) | collective-permute-done | bytes 131104 | tf_op jit(solution)/shard_map/ppermute | solution.py:14
  23.1 7.1 %collective-permute-done.1 = bf16[128,512]{1,0:T(8,128)(2,1)S(1)} collective-permute-done((bf16[128,512]{1,0:T(8,128)(2,1)S(1)}, bf16[128,512]{1,0:T(8,128)(2,1)S(1)}, u32[]{:S(2)}, u32[]{:S(2)}) %collective-permute-start.1) | collective-permute-done | bytes 131104 | tf_op jit(solution)/shard_map/ppermute | solution.py:14
  30.2 7.1 %collective-permute-done.2 = bf16[128,512]{1,0:T(8,128)(2,1)S(1)} collective-permute-done((bf16[128,512]{1,0:T(8,128)(2,1)S(1)}, bf16[128,512]{1,0:T(8,128)(2,1)S(1)}, u32[]{:S(2)}, u32[]{:S(2)}) %collective-permute-start.2) | collective-permute-done | bytes 131104 | tf_op jit(solution)/shard_map/ppermute | solution.py:14
  37.3 7.1 %collective-permute-done.3 = bf16[128,512]{1,0:T(8,128)(2,1)S(1)} collective-permute-done((bf16[128,512]{1,0:T(8,128)(2,1)S(1)}, bf16[128,512]{1,0:T(8,128)(2,1)S(1)}, u32[]{:S(2)}, u32[]{:S(2)}) %collective-permute-start.3) | collective-permute-done | bytes 131104 | tf_op jit(solution)/shard_map/ppermute | solution.py:14
  44.4 7.1 %collective-permute-done.4 = bf16[128,512]{1,0:T(8,128)(2,1)S(1)} collective-permute-done((bf16[128,512]{1,0:T(8,128)(2,1)S(1)}, bf16[128,512]{1,0:T(8,128)(2,1)S(1)}, u32[]{:S(2)}, u32[]{:S(2)}) %collective-permute-start.4) | collective-permute-done | bytes 131104 | tf_op jit(solution)/shard_map/ppermute | solution.py:14
  51.4 7.1 %collective-permute-done.5 = bf16[128,512]{1,0:T(8,128)(2,1)S(1)} collective-permute-done((bf16[128,512]{1,0:T(8,128)(2,1)S(1)}, bf16[128,512]{1,0:T(8,128)(2,1)S(1)}, u32[]{:S(2)}, u32[]{:S(2)}) %collective-permute-start.5) | collective-permute-done | bytes 131104 | tf_op jit(solution)/shard_map/ppermute | solution.py:14
  58.5 7.1 %collective-permute-done.6 = bf16[128,512]{1,0:T(8,128)(2,1)S(1)} collective-permute-done((bf16[128,512]{1,0:T(8,128)(2,1)S(1)}, bf16[128,512]{1,0:T(8,128)(2,1)S(1)}, u32[]{:S(2)}, u32[]{:S(2)}) %collective-permute-start.6) | collective-permute-done | bytes 131104 | tf_op jit(solution)/shard_map/ppermute | solution.py:14
  65.6 7.1 %collective-permute-done.7 = bf16[128,512]{1,0:T(8,128)(2,1)S(1)} collective-permute-done((bf16[128,512]{1,0:T(8,128)(2,1)S(1)}, bf16[128,512]{1,0:T(8,128)(2,1)S(1)}, u32[]{:S(2)}, u32[]{:S(2)}) %collective-permute-start.7) | collective-permute-done | bytes 131104 | tf_op jit(solution)/shard_map/ppermute | solution.py:14
  72.7 7.1 %collective-permute-done.8 = bf16[128,512]{1,0:T(8,128)(2,1)S(1)} collective-permute-done((bf16[128,512]{1,0:T(8,128)(2,1)S(1)}, bf16[128,512]{1,0:T(8,128)(2,1)S(1)}, u32[]{:S(2)}, u32[]{:S(2)}) %collective-permute-start.8) | collective-permute-done | bytes 131104 | tf_op jit(solution)/shard_map/ppermute | solution.py:14
  79.8 7.1 %collective-permute-done.9 = bf16[128,512]{1,0:T(8,128)(2,1)S(1)} collective-permute-done((bf16[128,512]{1,0:T(8,128)(2,1)S(1)}, bf16[128,512]{1,0:T(8,128)(2,1)S(1)}, u32[]{:S(2)}, u32[]{:S(2)}) %collective-permute-start.9) | collective-permute-done | bytes 131104 | tf_op jit(solution)/shard_map/ppermute | solution.py:14
  86.9 7.1 %collective-permute-done.10 = bf16[128,512]{1,0:T(8,128)(2,1)S(1)} collective-permute-done((bf16[128,512]{1,0:T(8,128)(2,1)S(1)}, bf16[128,512]{1,0:T(8,128)(2,1)S(1)}, u32[]{:S(2)}, u32[]{:S(2)}) %collective-permute-start.10) | collective-permute-done | bytes 131104 | tf_op jit(solution)/shard_map/ppermute | solution.py:14
  94.0 1.6 copy.80
  95.5 3.4 %all-to-all-start.2 = ((bf16[64,2,512]{2,0,1:T(8,128)(2,1)}), bf16[64,2,512]{2,0,1:T(8,128)(2,1)S(1)}, u32[]{:S(2)}, u32[]{:S(2)}) async-start(bf16[64,2,512]{2,0,1:T(8,128)(2,1)} %bitcast.99), calls=%async_computation.2 | async-start | bytes 262144 | tf_op jit(solution)/shard_map/all_to_all | solution.py:43
  98.9 1.9 copy.79
  100.8 3.2 %all-to-all-done.2 = bf16[64,2,512]{2,0,1:T(8,128)(2,1)S(1)} async-done(((bf16[64,2,512]{2,0,1:T(8,128)(2,1)}), bf16[64,2,512]{2,0,1:T(8,128)(2,1)S(1)}, u32[]{:S(2)}, u32[]{:S(2)}) %all-to-all-start.2) | async-done | bytes 131104 | tf_op jit(solution)/shard_map/all_to_all | solution.py:43
  104.0 3.5 %all-to-all-start = ((bf16[64,2,2048]{2,0,1:T(8,128)(2,1)}), bf16[64,2,2048]{2,0,1:T(8,128)(2,1)S(1)}, u32[]{:S(2)}, u32[]{:S(2)}) async-start(bf16[64,2,2048]{2,0,1:T(8,128)(2,1)} %bitcast.98), calls=%async_computation | async-start | bytes 1048576 | tf_op jit(solution)/shard_map/all_to_all | solution.py:41
  107.6 0.6 slice.29
  108.9 0.6 slice.26
  110.2 4.5 %collective-permute-done.12 = bf16[128,512]{1,0:T(8,128)(2,1)S(1)} collective-permute-done((bf16[128,512]{1,0:T(8,128)(2,1)S(1)}, bf16[128,512]{1,0:T(8,128)(2,1)S(1)}, u32[]{:S(2)}, u32[]{:S(2)}) %collective-permute-start.12) | collective-permute-done | bytes 131104 | tf_op jit(solution)/shard_map/ppermute | solution.py:14
  114.7 0.2 stack.41
  114.9 6.9 %collective-permute-done.13 = bf16[128,512]{1,0:T(8,128)(2,1)S(1)} collective-permute-done((bf16[128,512]{1,0:T(8,128)(2,1)S(1)}, bf16[128,512]{1,0:T(8,128)(2,1)S(1)}, u32[]{:S(2)}, u32[]{:S(2)}) %collective-permute-start.13) | collective-permute-done | bytes 131104 | tf_op jit(solution)/shard_map/ppermute | solution.py:14
  121.9 0.2 stack.42
  122.2 8.0 %collective-permute-done.14 = bf16[128,512]{1,0:T(8,128)(2,1)S(1)} collective-permute-done((bf16[128,512]{1,0:T(8,128)(2,1)S(1)}, bf16[128,512]{1,0:T(8,128)(2,1)S(1)}, u32[]{:S(2)}, u32[]{:S(2)}) %collective-permute-start.14) | collective-permute-done | bytes 131104 | tf_op jit(solution)/shard_map/ppermute | solution.py:14
  130.7 1.5 constant_dynamic-slice_fusion
  132.2 2.9 %copy.49 = bf16[2048,512]{0,1:T(8,128)(2,1)S(1)} copy(bf16[2048,512]{1,0:T(8,128)(2,1)} %constant_dynamic-slice_fusion) | data formatting | bytes 4194304 | tf_op jit(solution)/shard_map/jit(_roll_dynamic)/dynamic_slice | solution.py:17
  135.1 19.6 %all-gather.2.cloned.1.call-done = bf16[2048,512]{1,0:T(8,128)(2,1)} async-done(((bf16[128,512]{1,0:T(8,128)(2,1)}), bf16[2048,512]{1,0:T(8,128)(2,1)}) %all-gather.2.cloned.1.call-update) | async-done | bytes 2097168 | tf_op jit(solution)/shard_map/all_gather | solution.py:63
  154.8 4.0 %copy.51 = bf16[2048,512]{0,1:T(8,128)(2,1)} copy(bf16[2048,512]{1,0:T(8,128)(2,1)} %all-gather.2.cloned.1.call-done) | data formatting | bytes 4194304 | tf_op jit(solution)/shard_map/all_gather | solution.py:63
  158.8 8.9 %conditional.2 = (f32[1,64,4,4]{1,3,2,0:T(4,128)S(1)}, f32[1,64,2048]{2,1,0:T(8,128)S(1)}) conditional(s32[]{:T(128)} %bitcast.12, () %tuple.29, (s32[2048]{0:T(1024)S(1)}, s32[]{:T(128)}, s32[64]{0:T(128)S(1)}, bf16[2,64,4,4,128]{4,3,2,1,0:T(4,128)(2,1)S(1)}, bf16[2048,4,128]{0,2,1:T(8,128)(2,1)S(1)}, ...), branch_computations={%region_0.1_spmd, %region_1.4_spmd} | conditional | flops 1101134848 | bytes 42238768 | solution.py:81
  158.8 0.1 broadcast_compare_fusion
  159.1 1.7 fusion
  160.8 1.9 fusion.9
  162.7 2.5 %fusion.2 = f32[64,4,4]{0,2,1:T(4,128)S(1)} fusion(f32[4,2048,64,4]{1,2,3,0:T(8,128)S(1)} %get-tuple-element.106, f32[64,4,4]{0,2,1:T(4,128)S(1)} %broadcast_maximum_fusion, pred[64,2048]{1,0:T(8,128)(4,1)S(1)} %broadcast_compare_fusion), kind=kLoop, calls=%fused_computation.4 | loop fusion | flops 10484736 | bytes 8527872 | tf_op jit(solution)/shard_map/cond/branch_1_fun/reduce_sum | solution.py:28
  165.3 1.1 copy.45
  166.4 1.3 stack.31
  167.7 8.0 %conditional.3 = (f32[1,64,4,4]{1,3,2,0:T(4,128)S(1)}, f32[1,64,2048]{2,1,0:T(8,128)}) conditional(s32[]{:T(128)} %bitcast.20, () %tuple.31, (s32[2048]{0:T(1024)S(1)}, s32[]{:T(128)}, s32[64]{0:T(128)S(1)}, bf16[2,64,4,4,128]{4,3,2,1,0:T(4,128)(2,1)S(1)}, bf16[2048,4,128]{0,2,1:T(8,128)(2,1)S(1)}, /*index=5*/bf16[2048,4,128]{0,2,1:T(8,128)(2,1)}) %tuple.54), branch_computations={%region_4.5_spmd, %region_5.8_spmd} | conditional | flops 1101134848 | bytes 42238768 | solution.py:81
  168.2 1.7 fusion.17
  169.9 1.9 fusion.26
  171.8 2.5 %fusion.19 = f32[64,4,4]{0,2,1:T(4,128)S(1)} fusion(f32[4,2048,64,4]{1,2,3,0:T(8,128)S(1)} %get-tuple-element.108, f32[64,4,4]{0,2,1:T(4,128)S(1)} %broadcast_maximum_fusion.1, pred[64,2048]{1,0:T(8,128)(4,1)S(1)} %broadcast_compare_fusion.1), kind=kLoop, calls=%fused_computation.22 | loop fusion | flops 10484736 | bytes 8527872 | tf_op jit(solution)/shard_map/cond/branch_1_fun/reduce_sum | solution.py:28
  174.4 0.3 copy.46
  174.7 1.0 stack.35
  175.7 0.2 copy.58
  175.9 0.6 div.21
  176.5 0.4 div.22
  176.9 1.2 fusion.34
  178.2 11.1 %all_to_all.74 = bf16[2,64,2048]{2,1,0:T(8,128)(2,1)S(1)} all-to-all(bf16[2,64,2048]{2,1,0:T(8,128)(2,1)S(1)} %bitcast.106), channel_id=1, replica_groups=mesh['head'=2,'seq'=16] {'head'}, dimensions={0} | all-to-all | bytes 1048576 | tf_op jit(solution)/shard_map/all_to_all | solution.py:87
  189.3 0.8 copy.75
  (76 shorter events, 1.3 us)
Async XLA Ops:
  16.0 7.1 %collective-permute-start = (bf16[128,512]{1,0:T(8,128)(2,1)S(1)}, bf16[128,512]{1,0:T(8,128)(2,1)S(1)}, u32[]{:S(2)}, u32[]{:S(2)}) collective-permute-start(bf16[128,512]{1,0:T(8,128)(2,1)S(1)} %bitcast.108), channel_id=1, source_target_pairs={{0,1},{1,2},{2,3},{3,4},{4,5},{5,6},{6,7},{7,8},{8,9},{9,10},{10,1... | collective-permute-start | bytes 393224 | tf_op jit(solution)/shard_map/ppermute | solution.py:14
  23.1 7.1 %collective-permute-start.1 = (bf16[128,512]{1,0:T(8,128)(2,1)S(1)}, bf16[128,512]{1,0:T(8,128)(2,1)S(1)}, u32[]{:S(2)}, u32[]{:S(2)}) collective-permute-start(bf16[128,512]{1,0:T(8,128)(2,1)S(1)} %collective-permute-done), channel_id=1, source_target_pairs={{0,1},{1,2},{2,3},{3,4},{4,5},{5,6},{6,7},{7,8},{8,9},{9,10},{10,1... | collective-permute-start | bytes 393224 | tf_op jit(solution)/shard_map/ppermute | solution.py:14
  30.2 7.1 %collective-permute-start.2 = (bf16[128,512]{1,0:T(8,128)(2,1)S(1)}, bf16[128,512]{1,0:T(8,128)(2,1)S(1)}, u32[]{:S(2)}, u32[]{:S(2)}) collective-permute-start(bf16[128,512]{1,0:T(8,128)(2,1)S(1)} %collective-permute-done.1), channel_id=1, source_target_pairs={{0,1},{1,2},{2,3},{3,4},{4,5},{5,6},{6,7},{7,8},{8,9},{9,10},{10,1... | collective-permute-start | bytes 393224 | tf_op jit(solution)/shard_map/ppermute | solution.py:14
  37.3 7.1 %collective-permute-start.3 = (bf16[128,512]{1,0:T(8,128)(2,1)S(1)}, bf16[128,512]{1,0:T(8,128)(2,1)S(1)}, u32[]{:S(2)}, u32[]{:S(2)}) collective-permute-start(bf16[128,512]{1,0:T(8,128)(2,1)S(1)} %collective-permute-done.2), channel_id=1, source_target_pairs={{0,1},{1,2},{2,3},{3,4},{4,5},{5,6},{6,7},{7,8},{8,9},{9,10},{10,1... | collective-permute-start | bytes 393224 | tf_op jit(solution)/shard_map/ppermute | solution.py:14
  44.3 7.1 %collective-permute-start.4 = (bf16[128,512]{1,0:T(8,128)(2,1)S(1)}, bf16[128,512]{1,0:T(8,128)(2,1)S(1)}, u32[]{:S(2)}, u32[]{:S(2)}) collective-permute-start(bf16[128,512]{1,0:T(8,128)(2,1)S(1)} %collective-permute-done.3), channel_id=1, source_target_pairs={{0,1},{1,2},{2,3},{3,4},{4,5},{5,6},{6,7},{7,8},{8,9},{9,10},{10,1... | collective-permute-start | bytes 393224 | tf_op jit(solution)/shard_map/ppermute | solution.py:14
  51.4 7.1 %collective-permute-start.5 = (bf16[128,512]{1,0:T(8,128)(2,1)S(1)}, bf16[128,512]{1,0:T(8,128)(2,1)S(1)}, u32[]{:S(2)}, u32[]{:S(2)}) collective-permute-start(bf16[128,512]{1,0:T(8,128)(2,1)S(1)} %collective-permute-done.4), channel_id=1, source_target_pairs={{0,1},{1,2},{2,3},{3,4},{4,5},{5,6},{6,7},{7,8},{8,9},{9,10},{10,1... | collective-permute-start | bytes 393224 | tf_op jit(solution)/shard_map/ppermute | solution.py:14
  58.5 7.1 %collective-permute-start.6 = (bf16[128,512]{1,0:T(8,128)(2,1)S(1)}, bf16[128,512]{1,0:T(8,128)(2,1)S(1)}, u32[]{:S(2)}, u32[]{:S(2)}) collective-permute-start(bf16[128,512]{1,0:T(8,128)(2,1)S(1)} %collective-permute-done.5), channel_id=1, source_target_pairs={{0,1},{1,2},{2,3},{3,4},{4,5},{5,6},{6,7},{7,8},{8,9},{9,10},{10,1... | collective-permute-start | bytes 393224 | tf_op jit(solution)/shard_map/ppermute | solution.py:14
  65.6 7.1 %collective-permute-start.7 = (bf16[128,512]{1,0:T(8,128)(2,1)S(1)}, bf16[128,512]{1,0:T(8,128)(2,1)S(1)}, u32[]{:S(2)}, u32[]{:S(2)}) collective-permute-start(bf16[128,512]{1,0:T(8,128)(2,1)S(1)} %collective-permute-done.6), channel_id=1, source_target_pairs={{0,1},{1,2},{2,3},{3,4},{4,5},{5,6},{6,7},{7,8},{8,9},{9,10},{10,1... | collective-permute-start | bytes 393224 | tf_op jit(solution)/shard_map/ppermute | solution.py:14
  72.7 7.1 %collective-permute-start.8 = (bf16[128,512]{1,0:T(8,128)(2,1)S(1)}, bf16[128,512]{1,0:T(8,128)(2,1)S(1)}, u32[]{:S(2)}, u32[]{:S(2)}) collective-permute-start(bf16[128,512]{1,0:T(8,128)(2,1)S(1)} %collective-permute-done.7), channel_id=1, source_target_pairs={{0,1},{1,2},{2,3},{3,4},{4,5},{5,6},{6,7},{7,8},{8,9},{9,10},{10,1... | collective-permute-start | bytes 393224 | tf_op jit(solution)/shard_map/ppermute | solution.py:14
  79.8 7.1 %collective-permute-start.9 = (bf16[128,512]{1,0:T(8,128)(2,1)S(1)}, bf16[128,512]{1,0:T(8,128)(2,1)S(1)}, u32[]{:S(2)}, u32[]{:S(2)}) collective-permute-start(bf16[128,512]{1,0:T(8,128)(2,1)S(1)} %collective-permute-done.8), channel_id=1, source_target_pairs={{0,1},{1,2},{2,3},{3,4},{4,5},{5,6},{6,7},{7,8},{8,9},{9,10},{10,1... | collective-permute-start | bytes 393224 | tf_op jit(solution)/shard_map/ppermute | solution.py:14
  86.9 7.1 %collective-permute-start.10 = (bf16[128,512]{1,0:T(8,128)(2,1)S(1)}, bf16[128,512]{1,0:T(8,128)(2,1)S(1)}, u32[]{:S(2)}, u32[]{:S(2)}) collective-permute-start(bf16[128,512]{1,0:T(8,128)(2,1)S(1)} %collective-permute-done.9), channel_id=1, source_target_pairs={{0,1},{1,2},{2,3},{3,4},{4,5},{5,6},{6,7},{7,8},{8,9},{9,10},{10,1... | collective-permute-start | bytes 393224 | tf_op jit(solution)/shard_map/ppermute | solution.py:14
  94.0 13.6 %collective-permute-start.11 = (bf16[128,512]{1,0:T(8,128)(2,1)S(1)}, bf16[128,512]{1,0:T(8,128)(2,1)S(1)}, u32[]{:S(2)}, u32[]{:S(2)}) collective-permute-start(bf16[128,512]{1,0:T(8,128)(2,1)S(1)} %collective-permute-done.10), channel_id=1, source_target_pairs={{0,1},{1,2},{2,3},{3,4},{4,5},{5,6},{6,7},{7,8},{8,9},{9,10},{10,1... | collective-permute-start | bytes 393224 | tf_op jit(solution)/shard_map/ppermute | solution.py:14
  95.5 8.4 %all-to-all-start.2 = ((bf16[64,2,512]{2,0,1:T(8,128)(2,1)}), bf16[64,2,512]{2,0,1:T(8,128)(2,1)S(1)}, u32[]{:S(2)}, u32[]{:S(2)}) async-start(bf16[64,2,512]{2,0,1:T(8,128)(2,1)} %bitcast.99), calls=%async_computation.2 | async-start | bytes 262144 | tf_op jit(solution)/shard_map/all_to_all | solution.py:43
  104.0 6.1 %copy-start.2 = (bf16[64,2,512]{2,0,1:T(8,128)(2,1)}, bf16[64,2,512]{2,0,1:T(8,128)(2,1)S(1)}, u32[]{:S(2)}) copy-start(bf16[64,2,512]{2,0,1:T(8,128)(2,1)S(1)} %all-to-all-done.2) | copy-start | bytes 393220
  104.0 10.7 %all-to-all-start = ((bf16[64,2,2048]{2,0,1:T(8,128)(2,1)}), bf16[64,2,2048]{2,0,1:T(8,128)(2,1)S(1)}, u32[]{:S(2)}, u32[]{:S(2)}) async-start(bf16[64,2,2048]{2,0,1:T(8,128)(2,1)} %bitcast.98), calls=%async_computation | async-start | bytes 1048576 | tf_op jit(solution)/shard_map/all_to_all | solution.py:41
  107.5 47.3 %all-gather.2.cloned.1.call-start = ((), (), s32[]{:S(2)}) async-start(), calls=%async_computation.4 | async-start | bytes 2228224 | tf_op jit(solution)/shard_map/all_gather | solution.py:63
  107.5 7.1 %collective-permute-start.12 = (bf16[128,512]{1,0:T(8,128)(2,1)S(1)}, bf16[128,512]{1,0:T(8,128)(2,1)S(1)}, u32[]{:S(2)}, u32[]{:S(2)}) collective-permute-start(bf16[128,512]{1,0:T(8,128)(2,1)S(1)} %collective-permute-done.11), channel_id=1, source_target_pairs={{0,1},{1,2},{2,3},{3,4},{4,5},{5,6},{6,7},{7,8},{8,9},{9,10},{10,1... | collective-permute-start | bytes 393224 | tf_op jit(solution)/shard_map/ppermute | solution.py:14
  114.7 7.1 %collective-permute-start.13 = (bf16[128,512]{1,0:T(8,128)(2,1)S(1)}, bf16[128,512]{1,0:T(8,128)(2,1)S(1)}, u32[]{:S(2)}, u32[]{:S(2)}) collective-permute-start(bf16[128,512]{1,0:T(8,128)(2,1)S(1)} %collective-permute-done.12), channel_id=1, source_target_pairs={{0,1},{1,2},{2,3},{3,4},{4,5},{5,6},{6,7},{7,8},{8,9},{9,10},{10,1... | collective-permute-start | bytes 393224 | tf_op jit(solution)/shard_map/ppermute | solution.py:14
  121.8 8.3 %collective-permute-start.14 = (bf16[128,512]{1,0:T(8,128)(2,1)S(1)}, bf16[128,512]{1,0:T(8,128)(2,1)S(1)}, u32[]{:S(2)}, u32[]{:S(2)}) collective-permute-start(bf16[128,512]{1,0:T(8,128)(2,1)S(1)} %collective-permute-done.13), channel_id=1, source_target_pairs={{0,1},{1,2},{2,3},{3,4},{4,5},{5,6},{6,7},{7,8},{8,9},{9,10},{10,1... | collective-permute-start | bytes 393224 | tf_op jit(solution)/shard_map/ppermute | solution.py:14
  159.1 1.7 copy-start
  168.2 1.7 copy-start.1
Sparse Core Ops, SparseCore 0:
  110.5 44.2 all-gather.1
